TPU v7x, 256 devices: a whole 4x4x8 slice. The times are simulated.
256 devices in a mesh: dp: 64 (over z, y, core), vocab: 4 (over x).
Axes of the slice: x: 4, y: 4, z: 8, core: 2. Of those that a mesh axis runs over, the one named last changes fastest.
Arguments:
- hidden_in: bfloat16 [512, 24, 1024], P(('dp', 'vocab')), may hold values from -6 to 6
- tokens: int32 [512, 24], P(('dp', 'vocab')), may hold values from 0 to 131071
- lengths: int32 [512], P(('dp', 'vocab')), may hold values from 2 to 24, as said below
- cutoff: int32 [1], replicated, may hold values from 1 to 512
- norm_gain: float32 [1024], replicated, may hold values from 0.5 to 1.5
- gate_weight: bfloat16 [1024, 4096], P(None, 'vocab'), may hold values from -0.1875 to 0.1875
- up_weight: bfloat16 [1024, 4096], P(None, 'vocab'), may hold values from -0.1875 to 0.1875
- down_weight: bfloat16 [4096, 1024], P('vocab'), may hold values from -0.09375 to 0.09375
- final_gain: float32 [1024], replicated, may hold values from 0.5 to 1.5
- head_table: bfloat16 [131072, 1024], P(('dp', 'vocab')), may hold values from -12 to 12
Outputs:
- log_ppl: float32 [512], P(('dp', 'vocab'))
- margin: float32 [512], P(('dp', 'vocab'))
Inputs may be any that keep to these rules, and one draw needn't show every extreme that they name: Every length is 2 or more; the documents of one device have together at most 32 positions below their lengths, and some device has exactly 32.
All inputs are finite; a program needn't handle non-finite values.
Results may differ from a plain program's by a relative error of at most 0.025.
Values may be sent and summed in bfloat16 or wider, within the bound.
No kernel may reach another device: no remote copies, remote signals or barrier semaphores. Data moves between devices by JAX's collectives and lax.ppermute only.
A program may use at most 64 MiB of HBM per device.

v0:
```python
import jax
import jax.numpy as jnp
from jax import lax
from jax.sharding import Mesh
from jax.sharding import PartitionSpec as P

CAP = 32
DP = ("dp_0", "dp_1", "dp_2")
DP_VOCAB = ("dp_0", "dp_1", "dp_2", "vocab")


def copy_for_each(array, axis):
    length = lax.axis_size(axis)
    return lax.all_to_all(
        jnp.broadcast_to(array[None], (length, *array.shape)), axis, 0, 0, tiled=True
    )


def joined_along(parts, dim):
    parts = jnp.moveaxis(parts, 0, dim)
    lengths = parts.shape
    return parts.reshape(*lengths[:dim], lengths[dim] * lengths[dim + 1], *lengths[dim + 2 :])


def gather_directly(array, axis, dim):
    parts = copy_for_each(array, axis)
    return joined_along(parts, dim)


def split_up(array, dim, length):
    lengths = array.shape
    parts = array.reshape(*lengths[:dim], length, lengths[dim] // length, *lengths[dim + 1 :])
    return jnp.moveaxis(parts, dim, 0)


def sum_at_owner(array, axis, dim):
    parts = split_up(array, dim, lax.axis_size(axis))
    arrived = lax.all_to_all(parts, axis, split_axis=0, concat_axis=0, tiled=True)
    return arrived.sum(axis=0)


def all_in_one(array, axis):
    leaves = jax.tree.leaves(array)
    order = sorted(range(len(leaves)), key=lambda k: -leaves[k].size)
    width = (1, *leaves[order[0]].shape)[-1]
    lines = [
        jnp.pad(leaves[k].reshape(-1), (0, -leaves[k].size % width)).reshape(-1, width)
        for k in order
    ]
    both, at, found = (lax.all_gather(jnp.concatenate(lines), axis), 0, {})
    for k, line in zip(order, lines):
        share = both[:, at : at + len(line)].reshape(len(both), -1)
        found[k] = share[:, : leaves[k].size].reshape(-1, *leaves[k].shape)
        at += len(line)
    numbers = iter(range(len(leaves)))
    return jax.tree.map(lambda _: found[next(numbers)], array)


def joined_all(array, axes, combine):
    for axis in axes:
        pieces = all_in_one(array, axis)
        array = jax.tree.map(lambda part: part[0], pieces)
        for k in range(1, lax.axis_size(axis)):
            array = combine(array, jax.tree.map(lambda part: part[k], pieces))
    return array


def gathered_by_axis(array, axes, dim):
    far, near = axes
    parts = copy_for_each(copy_for_each(array, far), near)
    return joined_along(parts.swapaxes(0, 1).reshape(-1, *array.shape), dim)


def rms_norm(values, gain):
    squares = jnp.mean(values * values, axis=-1, keepdims=True)
    return values * lax.rsqrt(squares + 1e-06) * gain


def block_rows(row_count, shard_rows):
    shards = row_count // shard_rows
    grouped = 1
    for divisor in range(1, shards + 1):
        if shards % divisor == 0 and divisor * shard_rows <= 768:
            grouped = divisor
    return grouped * shard_rows


def merge_pair(left_side, right_side):
    highest = jnp.maximum(left_side[0], right_side[0])
    exp_sum = left_side[1] * jnp.exp(left_side[0] - highest) + right_side[1] * jnp.exp(
        right_side[0] - highest
    )
    return (highest, exp_sum, left_side[2] + right_side[2])


def make_accumulate(table, offset, shard_rows, model_width):
    column = jnp.arange(table.shape[0], dtype=jnp.int32)

    def score_block(block_pair):
        block_part, block_targets = block_pair
        logits = lax.dot_general(
            block_part, table, (((1,), (1,)), ((), ())), preferred_element_type=jnp.float32
        )
        highest = jnp.max(logits, axis=1)
        exp_sum = jnp.sum(jnp.exp(logits - highest[:, None]), axis=1)
        local_index = block_targets - offset
        picked = jnp.sum(jnp.where(column[None, :] == local_index[:, None], logits, 0.0), axis=1)
        return (highest, exp_sum, picked)

    def accumulate(running, segment, first_row):
        segment_rows, segment_targets = segment
        row_count = segment_rows.shape[0]
        block_size = block_rows(row_count, shard_rows)
        blocks = row_count // block_size
        results = lax.map(
            score_block,
            (
                segment_rows.reshape(blocks, block_size, model_width),
                segment_targets.reshape(blocks, block_size),
            ),
        )
        return tuple((fresh.reshape(row_count) for fresh in results))

    return accumulate


def on_device(
    hidden_in,
    tokens,
    lengths,
    cutoff,
    norm_gain,
    gate_weight,
    up_weight,
    down_weight,
    final_gain,
    head_table,
):
    doc_count, length, model_width = hidden_in.shape
    row_total = doc_count * length
    residual = hidden_in.reshape(row_total, model_width).astype(jnp.float32)
    normed = rms_norm(residual, norm_gain).astype(jnp.bfloat16)
    segment = gather_directly(normed, "vocab", 0)
    gate_part = jnp.dot(segment, gate_weight, preferred_element_type=jnp.float32)
    up_part = jnp.dot(segment, up_weight, preferred_element_type=jnp.float32)
    active = (jax.nn.silu(gate_part) * up_part).astype(jnp.bfloat16)
    branch = sum_at_owner(
        jnp.dot(active, down_weight, preferred_element_type=jnp.float32), "vocab", 0
    )
    stream = (residual + branch).astype(jnp.bfloat16)
    final_rows = rms_norm(stream.astype(jnp.float32), final_gain).astype(jnp.bfloat16)
    targets = jnp.concatenate([tokens[:, 1:], tokens[:, :1]], axis=1).reshape(row_total)
    position = jnp.arange(length, dtype=jnp.int32)
    live_mask = (position[None, :] < lengths[:, None] - 1).reshape(row_total)
    slot_index = jnp.cumsum(live_mask.astype(jnp.int32)) - 1
    placing = (slot_index[None, :] == jnp.arange(CAP, dtype=jnp.int32)[:, None]) & live_mask[
        None, :
    ]
    send_rows = jnp.dot(
        placing.astype(jnp.bfloat16), final_rows, preferred_element_type=jnp.float32
    ).astype(jnp.bfloat16)
    send_targets = jnp.sum(jnp.where(placing, targets[None, :], 0), axis=1)
    shard_rows = send_rows.shape[0]
    joined_table = gather_directly(head_table, "vocab", 0)
    offset = lax.axis_index(DP) * joined_table.shape[0]
    accumulate = make_accumulate(joined_table, offset, shard_rows, model_width)
    dp_rows = shard_rows * lax.axis_size(DP)
    blank_dp = jnp.zeros((dp_rows,), jnp.float32)
    peaks, sums_exp, picks = accumulate(
        (blank_dp, blank_dp, blank_dp),
        (
            lax.all_gather(send_rows, DP, axis=0, tiled=True),
            lax.all_gather(send_targets, DP, axis=0, tiled=True),
        ),
        jnp.int32(0),
    )
    peaks, sums_exp, picks = joined_all((peaks, sums_exp, picks), DP, merge_pair)
    mine = lax.axis_index(DP) * shard_rows
    highest = lax.dynamic_slice_in_dim(peaks, mine, shard_rows, 0)
    exp_sum = lax.dynamic_slice_in_dim(sums_exp, mine, shard_rows, 0)
    target_logit = lax.dynamic_slice_in_dim(picks, mine, shard_rows, 0)
    nll_slots = highest + jnp.log(exp_sum) - target_logit
    nll_rows = jnp.sum(jnp.where(placing, nll_slots[:, None], 0.0), axis=0)
    used_nll = jnp.where(live_mask, nll_rows, 0.0).reshape(doc_count, length)
    log_ppl = jnp.sum(used_nll, axis=1) / (lengths - 1).astype(jnp.float32)
    everyone = gathered_by_axis(log_ppl, (("dp_0", "dp_1"), ("dp_2", "vocab")), 0)
    ordered = jnp.sort(everyone)
    threshold = lax.dynamic_index_in_dim(ordered, cutoff[0] - 1, 0, keepdims=False)
    return (log_ppl, log_ppl - threshold)


def solution(mesh):
    finer = Mesh(
        mesh.devices.reshape(8, 4, 2, mesh.shape["vocab"]), ("dp_0", "dp_1", "dp_2", "vocab")
    )
    return jax.shard_map(
        on_device,
        mesh=finer,
        in_specs=(
            P(DP_VOCAB, None, None),
            P(DP_VOCAB, None),
            P(DP_VOCAB),
            P(),
            P(),
            P(None, "vocab"),
            P(None, "vocab"),
            P("vocab", None),
            P(),
            P(DP_VOCAB, None),
        ),
        out_specs=(P(DP_VOCAB), P(DP_VOCAB)),
        check_vma=False,
    )
```

profile of v0, /device:TPU:1, one launch (start us, length us, event | category | flops | bytes accessed | tf_op | source)
XLA Modules:
  0.0 228.5 jit_solution(5545836464481347392)
XLA Ops:
  7.2 1.1 fusion.14
  8.4 1.0 fusion.17
  9.5 11.8 %all_to_all.26 = bf16[4,48,1024]{2,1,0:T(8,128)(2,1)S(1)} all-to-all(bf16[4,48,1024]{2,1,0:T(8,128)(2,1)S(1)} %broadcast_in_dim.82), channel_id=1, replica_groups=mesh['dp_0'=8,'dp_1'=4,'dp_2'=2,'vocab'=4] {'vocab'}, dimensions={0} | all-to-all | bytes 786432 | tf_op jit(solution)/shard_map/all_to_all | solution.py:14
  21.3 0.6 fusion.78
  21.9 4.3 %fusion.7 = f32[192,1024]{1,0:T(8,128)} fusion(bf16[1024,1024]{1,0:T(8,128)(2,1)} %param.19, bf16[192,1024]{1,0:T(8,128)(2,1)S(1)} %bitcast.305, bf16[1024,1024]{1,0:T(8,128)(2,1)} %param.18, f32[192,1024]{1,0:T(8,128)S(1)} %fusion.78), kind=kOutput, calls=%fused_computation.11 | convolution fusion | flops 806486016 | bytes 6160384 | tf_op jit(solution)/shard_map/dot_general | solution.py:148
  26.2 3.5 %all-to-all-start.1 = ((f32[4,48,1024]{2,1,0:T(8,128)}), f32[4,48,1024]{2,1,0:T(8,128)S(1)}, u32[]{:S(2)}, u32[]{:S(2)}) async-start(f32[4,48,1024]{2,1,0:T(8,128)} %bitcast.306), calls=%async_computation.1 | async-start | bytes 1572864 | tf_op jit(solution)/shard_map/all_to_all | solution.py:38
  30.2 9.7 %all-to-all-done.1 = f32[4,48,1024]{2,1,0:T(8,128)S(1)} async-done(((f32[4,48,1024]{2,1,0:T(8,128)}), f32[4,48,1024]{2,1,0:T(8,128)S(1)}, u32[]{:S(2)}, u32[]{:S(2)}) %all-to-all-start.1) | async-done | bytes 786464 | tf_op jit(solution)/shard_map/all_to_all | solution.py:38
  40.2 0.9 convolution_convert_fusion
  41.1 3.7 %broadcast_in_dim.83 = bf16[4,512,1024]{2,1,0:T(8,128)(2,1)} broadcast(bf16[512,1024]{1,0:T(8,128)(2,1)} %param.21), dimensions={1,2} | broadcast | bytes 5242880 | tf_op jit(solution)/shard_map/broadcast_in_dim | solution.py:15
  44.9 5.0 %all-to-all-start.2 = ((bf16[4,512,1024]{2,1,0:T(8,128)(2,1)}), bf16[4,512,1024]{2,1,0:T(8,128)(2,1)}, u32[]{:S(2)}, u32[]{:S(2)}) async-start(bf16[4,512,1024]{2,1,0:T(8,128)(2,1)} %broadcast_in_dim.83), calls=%async_computation.2 | async-start | bytes 8388608 | tf_op jit(solution)/shard_map/all_to_all | solution.py:14
  51.8 23.7 %all-reduce = s32[2048]{0:T(1024)S(1)} all-reduce(s32[2048]{0:T(1024)S(1)} %dynamic-update-slice), channel_id=1, replica_groups=mesh['dp_0'=8,'dp_1'=4,'dp_2'=2,'vocab'=4] {'dp_0','dp_1','dp_2'}, use_global_device_ids=true, to_apply=%add | all-reduce | flops 2048 | bytes 16384
  75.5 20.4 %all-to-all-done.2 = bf16[4,512,1024]{2,1,0:T(8,128)(2,1)} async-done(((bf16[4,512,1024]{2,1,0:T(8,128)(2,1)}), bf16[4,512,1024]{2,1,0:T(8,128)(2,1)}, u32[]{:S(2)}, u32[]{:S(2)}) %all-to-all-start.2) | async-done | bytes 4194336 | tf_op jit(solution)/shard_map/all_to_all | solution.py:14
  95.8 28.5 %all-gather.8.cloned.1.call-done = bf16[2048,1024]{1,0:T(8,128)(2,1)} async-done(((bf16[32,1024]{1,0:T(8,128)(2,1)}), bf16[2048,1024]{1,0:T(8,128)(2,1)}) %all-gather.8.cloned.1.call-update) | async-done | bytes 4194320 | tf_op jit(solution)/shard_map/all_gather | solution.py:172
  124.3 26.3 %while.15 = (s32[]{:T(128)}, f32[4,512]{1,0:T(4,128)S(1)}, f32[4,512]{1,0:T(4,128)S(1)}, f32[4,512]{1,0:T(4,128)S(1)}, bf16[4,512,1024]{2,1,0:T(8,128)(2,1)}, /*...) while((s32[]{:T(128)}, f32[4,512]{1,0:T(4,128)S(1)}, ...), condition=%wide.region_9.10_spmd.clone, body=%wide.region_5.9_spmd.clone.sunk | while | flops 2153774080 | bytes 13658745 | solution.py:115
  124.3 5.0 %fusion.88 = (f32[512]{0:T(512)S(1)}, f32[512,2048]{1,0:T(8,128)S(1)}) fusion(bf16[2048,1024]{1,0:T(8,128)(2,1)} %get-tuple-element.189, bf16[4,512,1024]{2,1,0:T(8,128)(2,1)} %get-tuple-element.188, s32[]{:T(128)} %get-tuple-element.174), kind=kOutput, calls=%fused_computation.138.clone.1 | convolution fusion | flops 2148531712 | bytes 9439744 | tf_op jit(solution)/shard_map/while/body/eval_jaxpr/dot_general | solution.py:101
  129.3 1.4 select_reduce_fusion.5
  130.9 5.0 %fusion.88 = (f32[512]{0:T(512)S(1)}, f32[512,2048]{1,0:T(8,128)S(1)}) fusion(bf16[2048,1024]{1,0:T(8,128)(2,1)} %get-tuple-element.189, bf16[4,512,1024]{2,1,0:T(8,128)(2,1)} %get-tuple-element.188, s32[]{:T(128)} %get-tuple-element.174), kind=kOutput, calls=%fused_computation.138.clone.1 | convolution fusion | flops 2148531712 | bytes 9439744 | tf_op jit(solution)/shard_map/while/body/eval_jaxpr/dot_general | solution.py:101
  135.9 1.4 select_reduce_fusion.5
  137.5 5.0 %fusion.88 = (f32[512]{0:T(512)S(1)}, f32[512,2048]{1,0:T(8,128)S(1)}) fusion(bf16[2048,1024]{1,0:T(8,128)(2,1)} %get-tuple-element.189, bf16[4,512,1024]{2,1,0:T(8,128)(2,1)} %get-tuple-element.188, s32[]{:T(128)} %get-tuple-element.174), kind=kOutput, calls=%fused_computation.138.clone.1 | convolution fusion | flops 2148531712 | bytes 9439744 | tf_op jit(solution)/shard_map/while/body/eval_jaxpr/dot_general | solution.py:101
  142.4 1.4 select_reduce_fusion.5
  144.0 5.0 %fusion.88 = (f32[512]{0:T(512)S(1)}, f32[512,2048]{1,0:T(8,128)S(1)}) fusion(bf16[2048,1024]{1,0:T(8,128)(2,1)} %get-tuple-element.189, bf16[4,512,1024]{2,1,0:T(8,128)(2,1)} %get-tuple-element.188, s32[]{:T(128)} %get-tuple-element.174), kind=kOutput, calls=%fused_computation.138.clone.1 | convolution fusion | flops 2148531712 | bytes 9439744 | tf_op jit(solution)/shard_map/while/body/eval_jaxpr/dot_general | solution.py:101
  149.0 1.4 select_reduce_fusion.5
  150.7 18.4 %all-gather.3 = f32[8,3,2048]{2,1,0:T(4,128)S(1)} all-gather(f32[1,3,2048]{2,1,0:T(4,128)S(1)} %maximum_bitcast_fusion), channel_id=2, replica_groups=mesh['dp_0'=8,'dp_1'=4,'dp_2'=2,'vocab'=4] {'dp_0'}, dimensions={0}, use_global_device_ids=true | all-gather | bytes 221184 | tf_op jit(solution)/shard_map/all_gather | solution.py:50
  169.4 9.1 %all-gather.4 = f32[4,3,2048]{2,1,0:T(4,128)S(1)} all-gather(f32[1,3,2048]{2,1,0:T(4,128)S(1)} %maximum_bitcast_fusion.1), channel_id=3, replica_groups=mesh['dp_0'=8,'dp_1'=4,'dp_2'=2,'vocab'=4] {'dp_1'}, dimensions={0}, use_global_device_ids=true | all-gather | bytes 122880 | tf_op jit(solution)/shard_map/all_gather | solution.py:50
  178.7 11.2 %all-gather.5 = f32[2,3,2048]{2,1,0:T(4,128)S(1)} all-gather(f32[1,3,2048]{2,1,0:T(4,128)S(1)} %maximum_bitcast_fusion.2), channel_id=4, replica_groups=mesh['dp_0'=8,'dp_1'=4,'dp_2'=2,'vocab'=4] {'dp_2'}, dimensions={0}, use_global_device_ids=true | all-gather | bytes 73728 | tf_op jit(solution)/shard_map/all_gather | solution.py:50
  190.4 13.6 %all_to_all.27 = f32[32,1,2]{2,1,0:T(1,128)S(1)} all-to-all(f32[32,1,2]{2,1,0:T(1,128)S(1)} %broadcast_in_dim.90), channel_id=1, replica_groups=mesh['dp_0'=8,'dp_1'=4,'dp_2'=2,'vocab'=4] {'dp_0','dp_1'}, dimensions={0} | all-to-all | bytes 512 | tf_op jit(solution)/shard_map/all_to_all | solution.py:14
  204.1 0.6 broadcast_in_dim.92
  204.7 6.0 %all-to-all-start.4 = ((f32[8,32,2]{1,2,0:T(2,128)}), f32[8,32,2]{1,2,0:T(2,128)S(1)}, u32[]{:S(2)}, u32[]{:S(2)}) async-start(f32[8,32,2]{1,2,0:T(2,128)} %broadcast_in_dim.92), calls=%async_computation.4 | async-start | bytes 16384 | tf_op jit(solution)/shard_map/all_to_all | solution.py:14
  211.4 4.2 %all-to-all-done.4 = f32[8,32,2]{1,2,0:T(2,128)S(1)} async-done(((f32[8,32,2]{1,2,0:T(2,128)}), f32[8,32,2]{1,2,0:T(2,128)S(1)}, u32[]{:S(2)}, u32[]{:S(2)}) %all-to-all-start.4) | async-done | bytes 2080 | tf_op jit(solution)/shard_map/all_to_all | solution.py:14
  215.9 3.9 %sort.15 = (f32[512]{0:T(512)S(1)}, s32[512]{0:T(512)}) sort(f32[512]{0:T(512)S(1)} %reshape_reshape.3, s32[512]{0:T(512)S(1)} %iota.16), dimensions={0}, to_apply=%region_12.13 | sort | flops 4608 | bytes 8192 | tf_op jit(solution)/shard_map/jit(sort)/sort | solution.py:187
  219.8 0.7 dynamic_slice.27
  220.5 1.2 broadcast_subtract_fusion
  (79 shorter events, 4.1 us)
Async XLA Ops:
  7.2 14.1 %copy-start = (bf16[1024,1024]{1,0:T(8,128)(2,1)S(1)}, bf16[1024,1024]{1,0:T(8,128)(2,1)}, u32[]{:S(2)}) copy-start(bf16[1024,1024]{1,0:T(8,128)(2,1)} %param.17) | copy-start | bytes 6291460
  21.9 7.9 %copy-start.5 = (s32[2]{0:T(128)S(1)}, s32[2]{0:T(128)}, u32[]{:S(2)}) copy-start(s32[2]{0:T(128)} %param.14) | copy-start | bytes 28
  21.9 18.1 %copy-start.1 = (bf16[2,24,1024]{2,1,0:T(8,128)(2,1)S(1)}, bf16[2,24,1024]{2,1,0:T(8,128)(2,1)}, u32[]{:S(2)}) copy-start(bf16[2,24,1024]{2,1,0:T(8,128)(2,1)} %param.12) | copy-start | bytes 294916
  21.9 18.3 %copy-start.4 = (f32[1024]{0:T(1024)S(1)}, f32[1024]{0:T(1024)}, u32[]{:S(2)}) copy-start(f32[1024]{0:T(1024)} %param.20) | copy-start | bytes 12292
  26.2 13.7 %all-to-all-start.1 = ((f32[4,48,1024]{2,1,0:T(8,128)}), f32[4,48,1024]{2,1,0:T(8,128)S(1)}, u32[]{:S(2)}, u32[]{:S(2)}) async-start(f32[4,48,1024]{2,1,0:T(8,128)} %bitcast.306), calls=%async_computation.1 | async-start | bytes 1572864 | tf_op jit(solution)/shard_map/all_to_all | solution.py:38
  29.7 94.6 %all-gather.8.cloned.1.call-start = ((), (), s32[]{:S(2)}) async-start(), calls=%async_computation.5 | async-start | bytes 4259840 | tf_op jit(solution)/shard_map/all_gather | solution.py:172
  44.9 5.0 %copy-start.2 = (s32[2,24]{1,0:T(2,128)S(1)}, s32[2,24]{1,0:T(2,128)}, u32[]{:S(2)}) copy-start(s32[2,24]{1,0:T(2,128)} %param.13) | copy-start | bytes 580
  44.9 5.3 %copy-start.6 = (u32[256]{0:T(256)S(1)}, u32[256]{0:T(256)}, u32[]{:S(2)}) copy-start(u32[256]{0:T(256)} %constant.94) | copy-start | bytes 3076
  44.9 51.0 %all-to-all-start.2 = ((bf16[4,512,1024]{2,1,0:T(8,128)(2,1)}), bf16[4,512,1024]{2,1,0:T(8,128)(2,1)}, u32[]{:S(2)}, u32[]{:S(2)}) async-start(bf16[4,512,1024]{2,1,0:T(8,128)(2,1)} %broadcast_in_dim.83), calls=%async_computation.2 | async-start | bytes 8388608 | tf_op jit(solution)/shard_map/all_to_all | solution.py:14
  190.4 31.3 %copy-start.3 = (f32[2]{0:T(128)}, f32[2]{0:T(128)S(1)}, u32[]{:S(2)}) copy-start(f32[2]{0:T(128)S(1)} %convert_divide_fusion) | copy-start | bytes 28
  204.7 10.9 %all-to-all-start.4 = ((f32[8,32,2]{1,2,0:T(2,128)}), f32[8,32,2]{1,2,0:T(2,128)S(1)}, u32[]{:S(2)}, u32[]{:S(2)}) async-start(f32[8,32,2]{1,2,0:T(2,128)} %broadcast_in_dim.92), calls=%async_computation.4 | async-start | bytes 16384 | tf_op jit(solution)/shard_map/all_to_all | solution.py:14
Sparse Core Ops, SparseCore 0:
  41.2 83.0 all-gather.7
where the time goes:
time: 229 us
  blocking collectives  87.8 us (38%)
  waiting for transfers between devices  62.8 us (27%)
  matrix products  25.6 us (11%)
  between operations  15.7 us (7%)
  starting transfers between devices  14.6 us (6%)
  other arithmetic  14.4 us (6%)
  local copies, waits for them, and re-layouts  7.58 us (3%)
    all_gather x3, blocking collectives, all_in_one(): both, at, found = (lax.all_gather(jnp.concatenate(lines), axis), 0, {})  38.7 us
    all_gather x1, waiting for transfers between devices, on_device(): lax.all_gather(send_rows, DP, axis=0, tiled=True)  28.5 us
    all_to_all x2, blocking collectives, copy_for_each(): lax.all_to_all(jnp.broadcast_to(array[None], (length, *array.shape)), axi...  25.4 us
    all_to_all x2, waiting for transfers between devices, copy_for_each(): lax.all_to_all(jnp.broadcast_to(array[None], (length, *array.shape)), axi...  24.6 us
    unnamed x1, blocking collectives  23.7 us
    dot_general x4, matrix products, score_block(): lax.dot_general(block_part, table, (((1,), (1,)), ((), ())), preferred_el...  19.9 us
    all_to_all x2, starting transfers between devices, copy_for_each(): lax.all_to_all(jnp.broadcast_to(array[None], (length, *array.shape)), axi...  11 us
    all_to_all x1, waiting for transfers between devices, sum_at_owner(): lax.all_to_all(parts, axis, split_axis=0, concat_axis=0, tiled=True)  9.73 us
  transfers between devices with their start and end apart: 4, of which 4 were waited for; matrix products, arithmetic and copies ran while one was open for 2% of the time, Pallas kernels for 0%

commit v1 on v0

--- a/solution.py
+++ b/solution.py
@@ -169,7 +169,9 @@
     peaks, sums_exp, picks = accumulate(
         (blank_dp, blank_dp, blank_dp),
         (
-            lax.all_gather(send_rows, DP, axis=0, tiled=True),
+            jnp.concatenate(
+                lax.all_to_all(jnp.stack([send_rows] * lax.axis_size(DP)), DP, 0, 0), axis=0
+            ),
             lax.all_gather(send_targets, DP, axis=0, tiled=True),
         ),
         jnp.int32(0),

time: 229 us -> 306 us (1.34)
  blocking collectives: 87.8 us -> 179 us
  between operations: 15.7 us -> 2.25 us
  waiting for transfers between devices: 62.8 us -> 49.5 us
  starting transfers between devices: 14.6 us -> 25.6 us
    unnamed x1, blocking collectives: 23.7 us -> 97.1 us
    all_gather x1 -> x0, waiting for transfers between devices: 28.5 us -> none  [on_device(): lax.all_gather(send_rows, DP, axis=0, tiled=True)]
    all_to_all x2, waiting for transfers between devices: 24.6 us -> 49.5 us  [copy_for_each(): lax.all_to_all(jnp.broadcast_to(array[None], (length, *array.shape)), axi...]
    all_to_all x0 -> x1, blocking collectives: none -> 14 us  [sum_at_owner(): lax.all_to_all(parts, axis, split_axis=0, concat_axis=0, tiled=True)]
    all_to_all x1, starting transfers between devices: 3.49 us -> 15.5 us  [on_device(): lax.all_to_all(jnp.stack([send_rows] * lax.axis_size(DP)), DP, 0, 0)]
    all_to_all x1, waiting for transfers between devices: 9.73 us -> 0.01 us  [on_device(): lax.all_to_all(jnp.stack([send_rows] * lax.axis_size(DP)), DP, 0, 0)]
  transfers between devices with their start and end apart: 4 -> 3, of which waited for: 4 -> 2; matrix products, arithmetic and copies ran while one was open for 2% -> 1% of each run, Pallas kernels for 0% -> 0%
where the time goes in v1:
time: 306 us; the launch traced here: 305 us
  blocking collectives  179 us (58%)
  waiting for transfers between devices  49.5 us (16%)
  starting transfers between devices  25.6 us (8%)
  matrix products  24.8 us (8%)
  other arithmetic  14.4 us (5%)
  local copies, waits for them, and re-layouts  10.1 us (3%)
    unnamed x1, blocking collectives  97.1 us
    all_to_all x2, waiting for transfers between devices, copy_for_each(): lax.all_to_all(jnp.broadcast_to(array[None], (length, *array.shape)), axi...  49.5 us
    all_gather x3, blocking collectives, all_in_one(): both, at, found = (lax.all_gather(jnp.concatenate(lines), axis), 0, {})  40.7 us
    all_to_all x2, blocking collectives, copy_for_each(): lax.all_to_all(jnp.broadcast_to(array[None], (length, *array.shape)), axi...  26.9 us
    dot_general x4, matrix products, score_block(): lax.dot_general(block_part, table, (((1,), (1,)), ((), ())), preferred_el...  19.9 us
    all_to_all x1, starting transfers between devices, on_device(): lax.all_to_all(jnp.stack([send_rows] * lax.axis_size(DP)), DP, 0, 0)  15.5 us
    all_to_all x1, blocking collectives, sum_at_owner(): lax.all_to_all(parts, axis, split_axis=0, concat_axis=0, tiled=True)  14 us
    all_to_all x2, starting transfers between devices, copy_for_each(): lax.all_to_all(jnp.broadcast_to(array[None], (length, *array.shape)), axi...  10 us
  transfers between devices with their start and end apart: 3, of which 2 were waited for; matrix products, arithmetic and copies ran while one was open for 1% of the time, Pallas kernels for 0%

profile of v1, /device:TPU:1, one launch (start us, length us, event | category | flops | bytes accessed | tf_op | source)
XLA Modules:
  0.0 305.4 jit_solution(17548785909252117849)
XLA Ops:
  0.6 1.1 fusion.14
  1.9 1.0 fusion.17
  2.9 11.8 %all_to_all.31 = bf16[4,48,1024]{2,1,0:T(8,128)(2,1)S(1)} all-to-all(bf16[4,48,1024]{2,1,0:T(8,128)(2,1)S(1)} %broadcast_in_dim.82), channel_id=1, replica_groups=mesh['dp_0'=8,'dp_1'=4,'dp_2'=2,'vocab'=4] {'vocab'}, dimensions={0} | all-to-all | bytes 786432 | tf_op jit(solution)/shard_map/all_to_all | solution.py:14
  14.8 0.6 fusion.78
  15.3 4.2 %fusion.7 = f32[192,1024]{1,0:T(8,128)} fusion(bf16[1024,1024]{1,0:T(8,128)(2,1)} %param.19, bf16[192,1024]{1,0:T(8,128)(2,1)S(1)} %bitcast.305, bf16[1024,1024]{1,0:T(8,128)(2,1)} %param.18, f32[192,1024]{1,0:T(8,128)S(1)} %fusion.78), kind=kOutput, calls=%fused_computation.11 | convolution fusion | flops 806486016 | bytes 6160384 | tf_op jit(solution)/shard_map/dot_general | solution.py:148
  19.5 14.0 %all_to_all.32 = f32[4,48,1024]{2,1,0:T(8,128)S(1)} all-to-all(f32[4,48,1024]{2,1,0:T(8,128)} %bitcast.306), channel_id=1, replica_groups=mesh['dp_0'=8,'dp_1'=4,'dp_2'=2,'vocab'=4] {'vocab'}, dimensions={0} | all-to-all | bytes 1572864 | tf_op jit(solution)/shard_map/all_to_all | solution.py:38
  33.5 3.7 %broadcast_in_dim.83 = bf16[4,512,1024]{2,1,0:T(8,128)(2,1)} broadcast(bf16[512,1024]{1,0:T(8,128)(2,1)} %param.21), dimensions={1,2} | broadcast | bytes 5242880 | tf_op jit(solution)/shard_map/broadcast_in_dim | solution.py:15
  37.3 5.0 %all-to-all-start.3 = ((bf16[4,512,1024]{2,1,0:T(8,128)(2,1)}), bf16[4,512,1024]{2,1,0:T(8,128)(2,1)}, u32[]{:S(2)}, u32[]{:S(2)}) async-start(bf16[4,512,1024]{2,1,0:T(8,128)(2,1)} %broadcast_in_dim.83), calls=%async_computation.3 | async-start | bytes 8388608 | tf_op jit(solution)/shard_map/all_to_all | solution.py:14
  43.3 45.3 %all-to-all-done.3 = bf16[4,512,1024]{2,1,0:T(8,128)(2,1)} async-done(((bf16[4,512,1024]{2,1,0:T(8,128)(2,1)}), bf16[4,512,1024]{2,1,0:T(8,128)(2,1)}, u32[]{:S(2)}, u32[]{:S(2)}) %all-to-all-start.3) | async-done | bytes 4194336 | tf_op jit(solution)/shard_map/all_to_all | solution.py:14
  88.5 2.5 stack.2
  91.0 15.5 %all-to-all-start.2 = ((bf16[64,32,1024]{2,1,0:T(8,128)(2,1)}), bf16[64,32,1024]{2,1,0:T(8,128)(2,1)}, u32[]{:S(2)}, u32[]{:S(2)}) async-start(bf16[64,32,1024]{2,1,0:T(8,128)(2,1)} %stack.2), calls=%async_computation.2 | async-start | bytes 8388608 | tf_op jit(solution)/shard_map/all_to_all | solution.py:173
  106.9 0.6 dynamic-slice.1
  108.5 97.1 %all-reduce = s32[2048]{0:T(1024)S(1)} all-reduce(s32[2048]{0:T(1024)S(1)} %dynamic-update-slice), channel_id=1, replica_groups=mesh['dp_0'=8,'dp_1'=4,'dp_2'=2,'vocab'=4] {'dp_0','dp_1','dp_2'}, use_global_device_ids=true, to_apply=%add | all-reduce | flops 2048 | bytes 16384
  205.6 26.3 %while.15 = (s32[]{:T(128)}, f32[4,512]{1,0:T(4,128)S(1)}, f32[4,512]{1,0:T(4,128)S(1)}, f32[4,512]{1,0:T(4,128)S(1)}, bf16[4,512,1024]{2,1,0:T(8,128)(2,1)}, /*...) while((s32[]{:T(128)}, f32[4,512]{1,0:T(4,128)S(1)}, ...), condition=%wide.region_9.10_spmd.clone, body=%wide.region_5.9_spmd.clone.sunk | while | flops 2153774080 | bytes 13658745 | solution.py:115
  205.6 5.0 %fusion.88 = (f32[512]{0:T(512)S(1)}, f32[512,2048]{1,0:T(8,128)S(1)}) fusion(bf16[2048,1024]{1,0:T(8,128)(2,1)} %get-tuple-element.189, bf16[4,512,1024]{2,1,0:T(8,128)(2,1)} %get-tuple-element.188, s32[]{:T(128)} %get-tuple-element.174), kind=kOutput, calls=%fused_computation.138.clone.1 | convolution fusion | flops 2148531712 | bytes 9439744 | tf_op jit(solution)/shard_map/while/body/eval_jaxpr/dot_general | solution.py:101
  210.6 1.4 select_reduce_fusion.5
  212.2 5.0 %fusion.88 = (f32[512]{0:T(512)S(1)}, f32[512,2048]{1,0:T(8,128)S(1)}) fusion(bf16[2048,1024]{1,0:T(8,128)(2,1)} %get-tuple-element.189, bf16[4,512,1024]{2,1,0:T(8,128)(2,1)} %get-tuple-element.188, s32[]{:T(128)} %get-tuple-element.174), kind=kOutput, calls=%fused_computation.138.clone.1 | convolution fusion | flops 2148531712 | bytes 9439744 | tf_op jit(solution)/shard_map/while/body/eval_jaxpr/dot_general | solution.py:101
  217.2 1.4 select_reduce_fusion.5
  218.8 5.0 %fusion.88 = (f32[512]{0:T(512)S(1)}, f32[512,2048]{1,0:T(8,128)S(1)}) fusion(bf16[2048,1024]{1,0:T(8,128)(2,1)} %get-tuple-element.189, bf16[4,512,1024]{2,1,0:T(8,128)(2,1)} %get-tuple-element.188, s32[]{:T(128)} %get-tuple-element.174), kind=kOutput, calls=%fused_computation.138.clone.1 | convolution fusion | flops 2148531712 | bytes 9439744 | tf_op jit(solution)/shard_map/while/body/eval_jaxpr/dot_general | solution.py:101
  223.8 1.4 select_reduce_fusion.5
  225.4 5.0 %fusion.88 = (f32[512]{0:T(512)S(1)}, f32[512,2048]{1,0:T(8,128)S(1)}) fusion(bf16[2048,1024]{1,0:T(8,128)(2,1)} %get-tuple-element.189, bf16[4,512,1024]{2,1,0:T(8,128)(2,1)} %get-tuple-element.188, s32[]{:T(128)} %get-tuple-element.174), kind=kOutput, calls=%fused_computation.138.clone.1 | convolution fusion | flops 2148531712 | bytes 9439744 | tf_op jit(solution)/shard_map/while/body/eval_jaxpr/dot_general | solution.py:101
  230.4 1.4 select_reduce_fusion.5
  232.0 18.6 %all-gather.3 = f32[8,3,2048]{2,1,0:T(4,128)S(1)} all-gather(f32[1,3,2048]{2,1,0:T(4,128)S(1)} %maximum_bitcast_fusion), channel_id=2, replica_groups=mesh['dp_0'=8,'dp_1'=4,'dp_2'=2,'vocab'=4] {'dp_0'}, dimensions={0}, use_global_device_ids=true | all-gather | bytes 221184 | tf_op jit(solution)/shard_map/all_gather | solution.py:50
  250.9 9.4 %all-gather.4 = f32[4,3,2048]{2,1,0:T(4,128)S(1)} all-gather(f32[1,3,2048]{2,1,0:T(4,128)S(1)} %maximum_bitcast_fusion.1), channel_id=3, replica_groups=mesh['dp_0'=8,'dp_1'=4,'dp_2'=2,'vocab'=4] {'dp_1'}, dimensions={0}, use_global_device_ids=true | all-gather | bytes 122880 | tf_op jit(solution)/shard_map/all_gather | solution.py:50
  260.5 12.6 %all-gather.5 = f32[2,3,2048]{2,1,0:T(4,128)S(1)} all-gather(f32[1,3,2048]{2,1,0:T(4,128)S(1)} %maximum_bitcast_fusion.2), channel_id=4, replica_groups=mesh['dp_0'=8,'dp_1'=4,'dp_2'=2,'vocab'=4] {'dp_2'}, dimensions={0}, use_global_device_ids=true | all-gather | bytes 73728 | tf_op jit(solution)/shard_map/all_gather | solution.py:50
  273.7 15.1 %all_to_all.33 = f32[32,1,2]{2,1,0:T(1,128)S(1)} all-to-all(f32[32,1,2]{2,1,0:T(1,128)S(1)} %broadcast_in_dim.90), channel_id=1, replica_groups=mesh['dp_0'=8,'dp_1'=4,'dp_2'=2,'vocab'=4] {'dp_0','dp_1'}, dimensions={0} | all-to-all | bytes 512 | tf_op jit(solution)/shard_map/all_to_all | solution.py:14
  288.9 0.6 broadcast_in_dim.92
  289.5 5.0 %all-to-all-start.5 = ((f32[8,32,2]{1,2,0:T(2,128)}), f32[8,32,2]{1,2,0:T(2,128)S(1)}, u32[]{:S(2)}, u32[]{:S(2)}) async-start(f32[8,32,2]{1,2,0:T(2,128)} %broadcast_in_dim.92), calls=%async_computation.5 | async-start | bytes 16384 | tf_op jit(solution)/shard_map/all_to_all | solution.py:14
  295.2 4.2 %all-to-all-done.5 = f32[8,32,2]{1,2,0:T(2,128)S(1)} async-done(((f32[8,32,2]{1,2,0:T(2,128)}), f32[8,32,2]{1,2,0:T(2,128)S(1)}, u32[]{:S(2)}, u32[]{:S(2)}) %all-to-all-start.5) | async-done | bytes 2080 | tf_op jit(solution)/shard_map/all_to_all | solution.py:14
  299.7 3.9 %sort.15 = (f32[512]{0:T(512)S(1)}, s32[512]{0:T(512)}) sort(f32[512]{0:T(512)S(1)} %reshape_reshape.7, s32[512]{0:T(512)S(1)} %iota.16), dimensions={0}, to_apply=%region_12.13 | sort | flops 4608 | bytes 8192 | tf_op jit(solution)/shard_map/jit(sort)/sort | solution.py:189
  303.6 0.7 dynamic_slice.27
  304.2 1.2 broadcast_subtract_fusion
  (78 shorter events, 3.7 us)
Async XLA Ops:
  0.6 14.1 %copy-start = (bf16[1024,1024]{1,0:T(8,128)(2,1)S(1)}, bf16[1024,1024]{1,0:T(8,128)(2,1)}, u32[]{:S(2)}) copy-start(bf16[1024,1024]{1,0:T(8,128)(2,1)} %param.17) | copy-start | bytes 6291460
  37.3 5.0 %copy-start.5 = (s32[2]{0:T(128)S(1)}, s32[2]{0:T(128)}, u32[]{:S(2)}) copy-start(s32[2]{0:T(128)} %param.14) | copy-start | bytes 28
  37.3 5.5 %copy-start.1 = (bf16[2,24,1024]{2,1,0:T(8,128)(2,1)S(1)}, bf16[2,24,1024]{2,1,0:T(8,128)(2,1)}, u32[]{:S(2)}) copy-start(bf16[2,24,1024]{2,1,0:T(8,128)(2,1)} %param.12) | copy-start | bytes 294916
  37.3 5.8 %copy-start.4 = (f32[1024]{0:T(1024)S(1)}, f32[1024]{0:T(1024)}, u32[]{:S(2)}) copy-start(f32[1024]{0:T(1024)} %param.20) | copy-start | bytes 12292
  37.3 51.3 %all-to-all-start.3 = ((bf16[4,512,1024]{2,1,0:T(8,128)(2,1)}), bf16[4,512,1024]{2,1,0:T(8,128)(2,1)}, u32[]{:S(2)}, u32[]{:S(2)}) async-start(bf16[4,512,1024]{2,1,0:T(8,128)(2,1)} %broadcast_in_dim.83), calls=%async_computation.3 | async-start | bytes 8388608 | tf_op jit(solution)/shard_map/all_to_all | solution.py:14
  91.0 15.6 %copy-start.2 = (s32[2,24]{1,0:T(2,128)S(1)}, s32[2,24]{1,0:T(2,128)}, u32[]{:S(2)}) copy-start(s32[2,24]{1,0:T(2,128)} %param.13) | copy-start | bytes 580
  91.0 15.8 %copy-start.6 = (u32[256]{0:T(256)S(1)}, u32[256]{0:T(256)}, u32[]{:S(2)}) copy-start(u32[256]{0:T(256)} %constant.94) | copy-start | bytes 3076
  91.0 114.6 %all-to-all-start.2 = ((bf16[64,32,1024]{2,1,0:T(8,128)(2,1)}), bf16[64,32,1024]{2,1,0:T(8,128)(2,1)}, u32[]{:S(2)}, u32[]{:S(2)}) async-start(bf16[64,32,1024]{2,1,0:T(8,128)(2,1)} %stack.2), calls=%async_computation.2 | async-start | bytes 8388608 | tf_op jit(solution)/shard_map/all_to_all | solution.py:173
  273.7 31.8 %copy-start.3 = (f32[2]{0:T(128)}, f32[2]{0:T(128)S(1)}, u32[]{:S(2)}) copy-start(f32[2]{0:T(128)S(1)} %convert_divide_fusion) | copy-start | bytes 28
  289.5 9.9 %all-to-all-start.5 = ((f32[8,32,2]{1,2,0:T(2,128)}), f32[8,32,2]{1,2,0:T(2,128)S(1)}, u32[]{:S(2)}, u32[]{:S(2)}) async-start(f32[8,32,2]{1,2,0:T(2,128)} %broadcast_in_dim.92), calls=%async_computation.5 | async-start | bytes 16384 | tf_op jit(solution)/shard_map/all_to_all | solution.py:14
